TPU v7x, 8 devices: a whole 2x2x1 slice. The times are simulated.
8 devices in a mesh: data: 2 (over z, y), seq: 4 (over x, core).
Axes of the slice: x: 2, y: 2, z: 1, core: 2. Of those that a mesh axis runs over, the one named last changes fastest.
Arguments:
- tokens: bfloat16 [64, 4096, 768], P('data', 'seq'), parts along dimension 0
- lengths: int32 [64], P('data'), parts along dimension 0
- slot_params: bfloat16 [768, 128], replicated
- logit_scale: float32 [1], replicated
- w_in: bfloat16 [64, 768, 3072], P('seq')
- w_out: bfloat16 [64, 3072, 768], P('seq')
Outputs:
- output: bfloat16 [64, 4096, 768], P('data', 'seq'), parts along dimension 0
There are 2 independent parts. A program takes and returns all parts, laid end to end along the dimension named above; an argument that names none is the same for every part.
All inputs are finite; a program needn't handle non-finite values.
Results may differ from a plain program's by a relative error of at most 0.0148089.
Values are sent between devices in bfloat16 or wider.
A program may use at most 1 GiB of HBM per device.

v0:
```python
import jax
import jax.numpy as jnp
from jax import lax
from jax.sharding import PartitionSpec as P


def solution(mesh):
    seq_size = mesh.shape["seq"]

    def shard_body(tok_blk, len_blk, slot_params, logit_scale, w_in_blk, w_out_blk):
        num_rows, tok_count, model_width = tok_blk.shape
        num_slots = slot_params.shape[1]
        own_slots = num_slots // seq_size
        local_experts = w_in_blk.shape[0]
        slots_per = own_slots // local_experts
        shard_idx = lax.axis_index("seq")
        params_f32 = slot_params.astype(jnp.float32)
        col_inv = lax.rsqrt(jnp.sum(params_f32 * params_f32, axis=0, keepdims=True) + 1e-6)
        phi_norm = (params_f32 * (logit_scale[0] * col_inv)).astype(jnp.bfloat16)
        tok_f32 = tok_blk.astype(jnp.float32)
        tok_norm = (tok_f32 * lax.rsqrt(jnp.sum(tok_f32 * tok_f32, axis=-1, keepdims=True) + 1e-6)).astype(jnp.bfloat16)
        logits = jnp.einsum("btd,dn->btn", tok_norm, phi_norm, preferred_element_type=jnp.float32)
        positions = shard_idx * tok_count + jnp.arange(tok_count)
        is_valid = (positions[None, :] < len_blk[:, None])[:, :, None]
        local_max = jnp.max(jnp.where(is_valid, logits, -jnp.inf), axis=1)
        col_max = lax.pmax(local_max, "seq")
        disp_w = jnp.where(is_valid, jnp.exp(logits - col_max[:, None, :]), 0.0)
        col_sum = lax.psum(jnp.sum(disp_w, axis=1), "seq")
        part_sum = jnp.einsum("btn,btd->bnd", disp_w.astype(jnp.bfloat16), tok_blk, preferred_element_type=jnp.float32).astype(jnp.bfloat16)
        slot_sum = lax.psum_scatter(part_sum, "seq", scatter_dimension=1, tiled=True)
        own_sum = lax.dynamic_slice_in_dim(col_sum, shard_idx * own_slots, own_slots, axis=1)
        slot_in = (slot_sum.astype(jnp.float32) / own_sum[:, :, None]).astype(jnp.bfloat16)
        slot_in = slot_in.reshape(num_rows, local_experts, slots_per, model_width)
        hidden = jax.nn.gelu(jnp.einsum("besd,edf->besf", slot_in, w_in_blk, preferred_element_type=jnp.float32)).astype(jnp.bfloat16)
        slot_out = jnp.einsum("besf,efd->besd", hidden, w_out_blk, preferred_element_type=jnp.float32).astype(jnp.bfloat16)
        slot_out = slot_out.reshape(num_rows, own_slots, model_width)
        all_out = lax.all_gather(slot_out, "seq", axis=1, tiled=True)
        combine_w = jax.nn.softmax(logits, axis=-1).astype(jnp.bfloat16)
        mixed = jnp.einsum("btn,bnd->btd", combine_w, all_out, preferred_element_type=jnp.float32).astype(jnp.bfloat16)
        return jnp.where(is_valid, mixed, jnp.zeros_like(mixed))

    return jax.shard_map(
        shard_body,
        mesh=mesh,
        in_specs=(P("data", "seq", None), P("data"), P(None, None), P(None), P("seq", None, None), P("seq", None, None)),
        out_specs=P("data", "seq", None),
        check_vma=False,
    )
```

profile of v0, /device:TPU:0, one launch (start us, length us, event | category | flops | bytes accessed | tf_op | source)
XLA Modules:
  0.0 281.7 jit_solution(17591392680325609861)
XLA Ops:
  6.5 0.0 reduce-scatter.2.cloned.1.call-start
  7.2 1.0 fusion.34
  8.2 0.0 copy-start.1
  8.3 0.0 copy-start
  8.3 17.1 %fusion.1 = f32[32,1024]{1,0:T(8,128)S(1)} fusion(bf16[32,1024,768]{2,1,0:T(8,128)(2,1)} %param.6), kind=kLoop, calls=%fused_computation.3 | loop fusion | flops 75464704 | bytes 50462720 | tf_op jit(solution)/shard_map/reduce_sum | solution.py:21
  25.4 0.0 copy-done.1
  25.4 0.1 broadcast_compare_fusion
  25.5 0.0 copy-done
  25.5 23.5 %select_reduce_fusion = (f32[32,128]{1,0:T(8,128)S(1)}, f32[32,1024,128]{2,1,0:T(8,128)}) fusion(pred[32,1024]{1,0:T(8,128)(4,1)S(1)} %broadcast_compare_fusion, bf16[768,128]{1,0:T(8,128)(2,1)S(1)} %copy-done, f32[128]{0:T(128)S(1)} %rsqrt_multiply_fusion, bf16[32,1024,768]{2,1,0:T(8,128)(2,1)} %param.6, f32[32,1024]{1,0:T(8,128)S(1)} %add_rsqrt_fusion), kind=kOutput, calls=%fused_computation.14 | convolution fusion | flops 6526627840 | bytes 67486208 | tf_op jit(solution)/shard_map/btd,dn->btn/dot_general | solution.py:22
  49.0 13.0 %pmax.7 = f32[32,128]{1,0:T(8,128)S(1)} all-reduce(f32[32,128]{1,0:T(8,128)S(1)} %get-tuple-element.5), channel_id=1, replica_groups=mesh['data'=2,'seq'=4] {'seq'}, use_global_device_ids=true, to_apply=%region_5.6 | all-reduce | flops 4096 | bytes 32768 | tf_op jit(solution)/shard_map/pmax | solution.py:26
  62.0 26.0 %fusion.28 = bf16[32,128,768]{2,1,0:T(8,128)(2,1)} fusion(bf16[32,1024,768]{2,1,0:T(8,128)(2,1)} %param.6, f32[32,1024,128]{2,1,0:T(8,128)} %get-tuple-element.6, f32[32,128]{1,0:T(8,128)S(1)} %pmax.7, pred[32,1024]{1,0:T(8,128)(4,1)S(1)} %broadcast_compare_fusion), kind=kOutput, calls=%fused_computation.32 | convolution fusion | flops 6458179584 | bytes 73449472 | tf_op jit(solution)/shard_map/btn,btd->bnd/dot_general | solution.py:29
  88.1 0.0 reduce-scatter.2.cloned.1.call-update
  88.1 0.0 all-gather.2.cloned.1.call-start
  88.1 7.0 %fusion.10 = f32[32,128]{1,0:T(8,128)S(1)} fusion(f32[32,1024,128]{2,1,0:T(8,128)} %get-tuple-element.6, f32[32,128]{1,0:T(8,128)S(1)} %pmax.7, pred[32,1024]{1,0:T(8,128)(4,1)S(1)} %broadcast_compare_fusion), kind=kLoop, calls=%fused_computation.17 | loop fusion | flops 12578816 | bytes 16842752 | tf_op jit(solution)/shard_map/reduce_sum | solution.py:28
  95.2 10.4 %psum.7 = f32[32,128]{1,0:T(8,128)S(1)} all-reduce(f32[32,128]{1,0:T(8,128)S(1)} %fusion.10), channel_id=1, replica_groups=mesh['data'=2,'seq'=4] {'seq'}, use_global_device_ids=true, to_apply=%region_8.9 | all-reduce | flops 4096 | bytes 32768 | tf_op jit(solution)/shard_map/psum | solution.py:28
  105.6 0.1 constant_dynamic-slice_fusion
  105.7 34.0 %reduce-scatter.2.cloned.1.call-done = bf16[32,32,768]{2,1,0:T(8,128)(2,1)} async-done(((bf16[32,128,768]{2,1,0:T(8,128)(2,1)}), bf16[32,32,768]{2,1,0:T(8,128)(2,1)}) %reduce-scatter.2.cloned.1.call-update) | async-done | bytes 1572880 | tf_op jit(solution)/shard_map/reduce_scatter | solution.py:30
  139.7 1.8 divide_convert_fusion.2
  141.4 0.9 copy.13
  142.3 29.3 %fusion.19 = bf16[32,16,2,3072]{3,0,2,1:T(8,128)(2,1)} fusion(bf16[32,16,2,768]{3,0,2,1:T(8,128)(2,1)S(1)} %bitcast.37, bf16[16,768,3072]{2,1,0:T(8,128)(2,1)} %param.10), kind=kOutput, calls=%fused_computation.26 | convolution fusion | flops 4860149760 | bytes 83361792 | tf_op jit(solution)/shard_map/besd,edf->besf/dot_general | solution.py:34
  171.7 28.1 %fusion.31 = bf16[16,32,2,768]{3,1,2,0:T(8,128)(2,1)S(1)} fusion(bf16[32,16,2,3072]{3,0,2,1:T(8,128)(2,1)} %fusion.19, bf16[16,3072,768]{2,1,0:T(8,128)(2,1)} %param.11), kind=kOutput, calls=%fused_computation.34 | convolution fusion | flops 4832624640 | bytes 83361792 | tf_op jit(solution)/shard_map/besf,efd->besd/dot_general | solution.py:35
  199.8 2.0 copy.9
  201.8 0.0 all-gather.2.cloned.1.call-update
  201.8 22.2 %fusion.40 = (f32[32,1024]{1,0:T(8,128)S(1)}, f32[32,1024,128]{2,1,0:T(8,128)}) fusion(f32[32,1024,128]{2,1,0:T(8,128)} %get-tuple-element.6), kind=kOutput, calls=%fused_computation.47 | output fusion | flops 8388735 | bytes 33685504 | tf_op jit(solution)/shard_map/sub | solution.py:38
  224.1 21.6 %all-gather.2.cloned.1.call-done = bf16[32,128,768]{2,1,0:T(8,128)(2,1)} async-done(((bf16[32,32,768]{2,1,0:T(8,128)(2,1)}), bf16[32,128,768]{2,1,0:T(8,128)(2,1)}) %all-gather.2.cloned.1.call-update) | async-done | bytes 6291472 | tf_op jit(solution)/shard_map/all_gather | solution.py:37
  245.6 29.3 %convert_select_fusion = bf16[32,1024,768]{2,1,0:T(8,128)(2,1)} fusion(pred[32,1024]{1,0:T(8,128)(4,1)S(1)} %broadcast_compare_fusion, bf16[32,128,768]{2,1,0:T(8,128)(2,1)} %all-gather.2.cloned.1.call-done, f32[32,1024,128]{2,1,0:T(8,128)} %get-tuple-element.8, f32[32,1024]{1,0:T(8,128)S(1)} %get-tuple-element.7), kind=kOutput, calls=%fused_computation.10 | convolution fusion | flops 6501171200 | bytes 73564160 | tf_op jit(solution)/shard_map/btn,bnd->btd/dot_general | solution.py:39
  (3 shorter events, 0.0 us)
Async XLA Ops:
  6.5 133.1 %reduce-scatter.2.cloned.1.call-start = ((), (), s32[]{:S(2)}) async-start(), calls=%async_computation.1 | async-start | bytes 7864320 | tf_op jit(solution)/shard_map/reduce_scatter | solution.py:30
  8.2 17.1 %copy-start.1 = (s32[32]{0:T(128)S(1)}, s32[32]{0:T(128)}, u32[]{:S(2)}) copy-start(s32[32]{0:T(128)} %param.7) | copy-start | bytes 388
  8.3 17.2 %copy-start = (bf16[768,128]{1,0:T(8,128)(2,1)S(1)}, bf16[768,128]{1,0:T(8,128)(2,1)}, u32[]{:S(2)}) copy-start(bf16[768,128]{1,0:T(8,128)(2,1)} %param.8) | copy-start | bytes 589828
  88.1 157.5 %all-gather.2.cloned.1.call-start = ((), (), s32[]{:S(2)}) async-start(), calls=%async_computation.2 | async-start | bytes 7864320 | tf_op jit(solution)/shard_map/all_gather | solution.py:37
Sparse Core Ops, SparseCore 0:
  88.2 51.4 reduce-scatter.1
  201.9 43.6 all-gather.1
where the time goes:
time: 282 us
  matrix products  136 us (48%)
  waiting for transfers between devices  55.6 us (20%)
  other arithmetic  49.2 us (17%)
  blocking collectives  23.5 us (8%)
  between operations  14.1 us (5%)
  local copies, waits for them, and re-layouts  2.96 us (1%)
    reduce_scatter x1, waiting for transfers between devices, shard_body(): lax.psum_scatter(part_sum, 'seq', scatter_dimension=1, tiled=True)  34 us
    dot_general x1, matrix products, shard_body(): jnp.einsum('besd,edf->besf', slot_in, w_in_blk, preferred_element_type=jn...  29.3 us
    dot_general x1, matrix products, shard_body(): jnp.einsum('btn,bnd->btd', combine_w, all_out, preferred_element_type=jnp...  29.3 us
    dot_general x1, matrix products, shard_body(): jnp.einsum('besf,efd->besd', hidden, w_out_blk, preferred_element_type=jn...  28.1 us
    dot_general x1, matrix products, shard_body(): jnp.einsum('btn,btd->bnd', disp_w.astype(jnp.bfloat16), tok_blk, preferre...  26 us
    dot_general x1, matrix products, shard_body(): jnp.einsum('btd,dn->btn', tok_norm, phi_norm, preferred_element_type=jnp....  23.5 us
    sub x1, other arithmetic, shard_body(): combine_w = jax.nn.softmax(logits, axis=-1).astype(jnp.bfloat16)  22.2 us
    all_gather x1, waiting for transfers between devices, shard_body(): all_out = lax.all_gather(slot_out, 'seq', axis=1, tiled=True)  21.6 us
  transfers between devices with their start and end apart: 2, of which 2 were waited for; matrix products, arithmetic and copies ran while one was open for 10% of the time, Pallas kernels for 0%

commit v1 on v0

v1 whole, which is shorter than its diff:
```python
import functools

import jax
import jax.numpy as jnp
from jax import lax
from jax.experimental import pallas as pl
from jax.experimental.pallas import tpu as pltpu
from jax.sharding import PartitionSpec as P

BLK = 256
TS = 4
WS = 4
FC = 512
G = 16


def _swap_matrix():
    r = lax.broadcasted_iota(jnp.int32, (G * G, G * G), 0)
    c = lax.broadcasted_iota(jnp.int32, (G * G, G * G), 1)
    hit = ((r >> 4) == (c & 15)) & ((r & 15) == (c >> 4))
    return jnp.where(hit, 1.0, 0.0).astype(jnp.bfloat16)


def _front_kernel(rows, experts, len_ref, scale_ref, phi_ref, x_hbm, win_hbm, wout_hbm,
                  ys_hbm, ct_hbm,
                  xbuf, phit, wt, ctst, sbuf, rbuf, qbuf, xst, zt, zr, zs, yst, w1, w2,
                  tok_sem, ct_sem, w_sem, z_ssem, z_rsem,
                  d_ssem, d_rsem, x_ssem, x_rsem,
                  l_sem, c_ssem, c_rsem, p_ssem, p_rsem, f_ssem, f_rsem):
    toks, width = x_hbm.shape[1], x_hbm.shape[2]
    slots = phi_ref.shape[1]
    own = sbuf.shape[3]
    per = own // experts
    me = lax.axis_index("seq")
    xi = me // 2
    ci = me % 2
    core_peer = 2 * xi + (1 - ci)
    x_peer = 2 * (1 - xi) + ci
    diag = 2 * (1 - xi) + (1 - ci)

    def remote(src, dst, ssem, rsem, dev):
        return pltpu.make_async_remote_copy(
            src_ref=src, dst_ref=dst, send_sem=ssem, recv_sem=rsem,
            device_id={"seq": dev}, device_id_type=pl.DeviceIdType.MESH)

    def tok_copy(b):
        return pltpu.make_async_copy(x_hbm.at[b], xbuf.at[b % TS], tok_sem.at[b % TS])

    def ct_copy(b):
        return pltpu.make_async_copy(ctst.at[b % 2], ct_hbm.at[b], ct_sem.at[b % 2])

    def w1_copy(e):
        return pltpu.make_async_copy(win_hbm.at[e], w1.at[e % WS], w_sem.at[e % WS, 0])

    def w2_copy(e):
        return pltpu.make_async_copy(wout_hbm.at[e], w2.at[e % WS], w_sem.at[e % WS, 1])

    def d_copy(b):
        return remote(sbuf.at[b, :, 1 - ci], rbuf.at[b], d_ssem.at[b], d_rsem.at[b], core_peer)

    def x_copy(b):
        return remote(rbuf.at[b, 1 - xi], qbuf.at[b], x_ssem.at[b], x_rsem.at[b], x_peer)

    def z_copies():
        out = []
        for k, dev in enumerate((core_peer, x_peer, diag)):
            out.append(remote(zt.at[pl.ds(pl.multiple_of(dev * own, own), own)], zr.at[k],
                              z_ssem.at[k], z_rsem.at[k], dev))
        return out

    barrier = pltpu.get_barrier_semaphore()
    for dev in (core_peer, x_peer, diag):
        pl.semaphore_signal(barrier, inc=1, device_id={"seq": dev}, device_id_type=pl.DeviceIdType.MESH)
    for k in range(TS - 1):
        tok_copy(k).start()

    scale = scale_ref[0]
    phi = phi_ref[...].astype(jnp.float32)
    col_inv = lax.rsqrt(jnp.sum(phi * phi, axis=0, keepdims=True) + 1e-6)
    phit[...] = (phi * (scale * col_inv)).T.astype(jnp.bfloat16)
    zt[...] = jnp.zeros_like(zt)

    def gate(b):
        limit = len_ref[b] - me * toks
        zacc = None
        for k in range(toks // BLK):
            cols = pl.ds(k * BLK, BLK)
            xf = xbuf[b % TS, cols, :].astype(jnp.float32)
            inv = lax.rsqrt(jnp.sum(xf * xf, axis=1, keepdims=True) + 1e-6)
            xn = (xf * inv).astype(jnp.bfloat16)
            lt = lax.dot_general(phit[...], xn, (((1,), (1,)), ((), ())),
                                 preferred_element_type=jnp.float32)
            e = jnp.exp(lt - scale)
            den = jnp.sum(e, axis=0, keepdims=True)
            ctst[b % 2, :, cols] = (e * (1.0 / den)).astype(jnp.bfloat16)
            pos = lax.broadcasted_iota(jnp.int32, (1, BLK), 1) + k * BLK
            w = jnp.where(pos < limit, e, 0.0)
            wt[:, cols] = w.astype(jnp.bfloat16)
            for h in range(BLK // 128):
                part = w[:, h * 128:(h + 1) * 128]
                zacc = part if zacc is None else zacc + part
        zcol = jnp.sum(zacc, axis=1, keepdims=True)
        lane = lax.broadcasted_iota(jnp.int32, zt.shape, 1)
        zt[...] = jnp.where(lane == b, zcol, zt[...])

    def sums(b):
        s = jnp.dot(wt[...], xbuf[b % TS], preferred_element_type=jnp.float32)
        sbuf[b] = s.astype(jnp.bfloat16).reshape(2, 2, own, width)

    def mid(b):
        for h in range(2):
            rbuf[b, h] = (rbuf[b, h].astype(jnp.float32)
                          + sbuf[b, h, ci].astype(jnp.float32)).astype(jnp.bfloat16)

    tok_copy(0).wait()
    gate(0)
    ct_copy(0).start()
    pl.semaphore_wait(barrier, 3)

    def step(b, _):
        @pl.when(b >= 2)
        def _():
            d_copy(b - 2).start()

        @pl.when(b >= 5)
        def _():
            x_copy(b - 5).start()

        @pl.when(b >= 4)
        def _():
            d_copy(b - 4).wait_recv()
            mid(b - 4)

        @pl.when(b >= 2)
        def _():
            ct_copy(b - 2).wait()

        @pl.when(b + TS - 2 < rows)
        def _():
            tok_copy(b + TS - 2).start()

        for k in range(2 * WS):
            @pl.when(b == 3 * k + 2)
            def _():
                (w2_copy if k % 2 else w1_copy)(k // 2).start()

        tok_copy(b).wait()
        sums(b - 1)
        gate(b)
        ct_copy(b).start()
        return 0

    lax.fori_loop(1, rows, step, 0)
    zc = z_copies()
    for z in zc:
        z.start()
    d_copy(rows - 2).start()
    x_copy(rows - 5).start()
    sums(rows - 1)
    d_copy(rows - 4).wait_recv()
    mid(rows - 4)
    d_copy(rows - 1).start()
    d_copy(rows - 3).wait_recv()
    mid(rows - 3)
    x_copy(rows - 4).start()
    d_copy(rows - 2).wait_recv()
    mid(rows - 2)
    x_copy(rows - 3).start()
    d_copy(rows - 1).wait_recv()
    mid(rows - 1)
    x_copy(rows - 2).start()
    ct_copy(rows - 2).wait()
    ct_copy(rows - 1).wait()
    for z in zc:
        z.wait_recv()
    x_copy(rows - 1).start()

    zs[...] = jnp.ones_like(zs)
    zs[:own, :] = zt[pl.ds(pl.multiple_of(me * own, own), own), :] + zr[0] + zr[1] + zr[2]
    zs[...] = 1.0 / zs[...].T

    swap = _swap_matrix()
    for h in range(rows // G):
        def wait_x(i, _):
            x_copy(i).wait_recv()
            return 0
        lax.fori_loop(h * G, (h + 1) * G, wait_x, 0)
        for g in range(own // G):
            near = rbuf[pl.ds(h * G, G), xi, pl.ds(g * G, G), :].reshape(G * G, width)
            far = qbuf[pl.ds(h * G, G), pl.ds(g * G, G), :].reshape(G * G, width)
            s = (jnp.dot(swap, near, preferred_element_type=jnp.float32)
                 + jnp.dot(swap, far, preferred_element_type=jnp.float32))
            for k in range(G):
                zinv = zs[h * G:(h + 1) * G, g * G + k:g * G + k + 1]
                xst[g * G + k, pl.ds(h * G, G), :] = (s[k * G:(k + 1) * G] * zinv).astype(jnp.bfloat16)

    def at(dev, e):
        return ys_hbm.at[pl.ds(dev * own + e * per, per)]

    def l_copy(e):
        return pltpu.make_async_copy(yst.at[e], at(me, e), l_sem.at[e])

    def c_copy(e):
        return remote(yst.at[e], at(me, e), c_ssem.at[e], c_rsem.at[e], core_peer)

    def p_copy(e):
        return remote(yst.at[e], at(me, e), p_ssem.at[e], p_rsem.at[e], x_peer)

    def f_copy(e):
        return remote(at(x_peer, e), at(x_peer, e), f_ssem.at[e], f_rsem.at[e], core_peer)

    def send(e):
        p_copy(e).start()
        c_copy(e).start()
        l_copy(e).start()

    def expert(e, _):
        @pl.when(e >= 1)
        def _():
            send(e - 1)

        @pl.when(e >= 4)
        def _():
            p_copy(e - 4).wait_recv()
            f_copy(e - 4).start()

        w1_copy(e).wait()
        w2_copy(e).wait()
        slot = e % WS
        xs = xst[pl.ds(e * per, per)].reshape(per * rows, width)
        acc = None
        for f in range(w1.shape[2] // FC):
            hid = jnp.dot(xs, w1[slot, :, f * FC:(f + 1) * FC], preferred_element_type=jnp.float32)
            hid = jax.nn.gelu(hid).astype(jnp.bfloat16)
            part = jnp.dot(hid, w2[slot, f * FC:(f + 1) * FC, :], preferred_element_type=jnp.float32)
            acc = part if acc is None else acc + part
        yst[e] = acc.astype(jnp.bfloat16).reshape(per, rows, width)

        @pl.when(e + WS < experts)
        def _():
            w1_copy(e + WS).start()
            w2_copy(e + WS).start()

        return 0

    lax.fori_loop(0, experts, expert, 0)

    def drain(b, _):
        d_copy(b).wait_send()
        x_copy(b).wait_send()
        return 0
    lax.fori_loop(0, rows, drain, 0)
    for z in zc:
        z.wait_send()
    send(experts - 1)
    for e in range(experts - 4, experts):
        p_copy(e).wait_recv()
        f_copy(e).start()

    def finish(e, _):
        l_copy(e).wait()
        c_copy(e).wait()
        p_copy(e).wait_send()
        f_copy(e).wait()
        return 0
    lax.fori_loop(0, experts, finish, 0)


def _combine_kernel(len_ref, ct_ref, ys_ref, y_ref, ysb):
    b = pl.program_id(0)
    toks, width = y_ref.shape[1], y_ref.shape[2]
    slots = ys_ref.shape[0]

    @pl.when(b % G == 0)
    def _():
        swap = _swap_matrix()
        for g in range(slots // G):
            blk = ys_ref[pl.ds(g * G, G)].reshape(G * G, width)
            out = jnp.dot(swap, blk, preferred_element_type=jnp.float32).astype(jnp.bfloat16)
            ysb[:, pl.ds(g * G, G), :] = out.reshape(G, G, width)

    limit = len_ref[b] - lax.axis_index("seq") * toks
    own = ysb[b % G]
    for k in range(toks // BLK):
        c = ct_ref[0, :, k * BLK:(k + 1) * BLK]
        mixed = lax.dot_general(c, own, (((0,), (0,)), ((), ())), preferred_element_type=jnp.float32)
        pos = lax.broadcasted_iota(jnp.int32, (BLK, 1), 0) + k * BLK
        y_ref[0, k * BLK:(k + 1) * BLK, :] = jnp.where(pos < limit, mixed, 0.0).astype(jnp.bfloat16)


def solution(mesh):
    def shard_body(tok_blk, len_blk, slot_params, logit_scale, w_in_blk, w_out_blk):
        rows, toks, width = tok_blk.shape
        slots = slot_params.shape[1]
        experts, _, ff = w_in_blk.shape
        own = slots // mesh.shape["seq"]
        per = own // experts
        bf, f32 = jnp.bfloat16, jnp.float32
        any_spec = pl.BlockSpec(memory_space=pl.ANY)
        smem = pl.BlockSpec(memory_space=pltpu.SMEM)
        dma = pltpu.SemaphoreType.DMA
        ys, ct = pl.pallas_call(
            functools.partial(_front_kernel, rows, experts),
            out_shape=(jax.ShapeDtypeStruct((slots, rows, width), bf),
                       jax.ShapeDtypeStruct((rows, slots, toks), bf)),
            in_specs=[smem, smem, pl.BlockSpec(memory_space=pltpu.VMEM), any_spec, any_spec, any_spec],
            out_specs=(any_spec, any_spec),
            scratch_shapes=[
                pltpu.VMEM((TS, toks, width), bf),
                pltpu.VMEM((slots, width), bf),
                pltpu.VMEM((slots, toks), bf),
                pltpu.VMEM((2, slots, toks), bf),
                pltpu.VMEM((rows, 2, 2, own, width), bf),
                pltpu.VMEM((rows, 2, own, width), bf),
                pltpu.VMEM((rows, own, width), bf),
                pltpu.VMEM((own, rows, width), bf),
                pltpu.VMEM((slots, 128), f32),
                pltpu.VMEM((3, own, 128), f32),
                pltpu.VMEM((128, 128), f32),
                pltpu.VMEM((experts, per, rows, width), bf),
                pltpu.VMEM((WS, width, ff), bf),
                pltpu.VMEM((WS, ff, width), bf),
                dma((TS,)), dma((2,)), dma((WS, 2)), dma((3,)), dma((3,)),
                dma((rows,)), dma((rows,)), dma((rows,)), dma((rows,)),
                dma((experts,)), dma((experts,)), dma((experts,)), dma((experts,)),
                dma((experts,)), dma((experts,)), dma((experts,)),
            ],
            compiler_params=pltpu.CompilerParams(
                collective_id=0, has_side_effects=True, vmem_limit_bytes=67_000_000),
            name="front",
        )(len_blk, logit_scale, slot_params, tok_blk, w_in_blk, w_out_blk)
        return pl.pallas_call(
            _combine_kernel,
            grid_spec=pltpu.PrefetchScalarGridSpec(
                num_scalar_prefetch=1,
                grid=(rows,),
                in_specs=[
                    pl.BlockSpec((1, slots, toks), lambda b, n: (b, 0, 0)),
                    pl.BlockSpec((slots, G, width), lambda b, n: (0, b // G, 0)),
                ],
                out_specs=pl.BlockSpec((1, toks, width), lambda b, n: (b, 0, 0)),
                scratch_shapes=[pltpu.VMEM((G, slots, width), bf)],
            ),
            out_shape=jax.ShapeDtypeStruct((rows, toks, width), bf),
            compiler_params=pltpu.CompilerParams(vmem_limit_bytes=60_000_000),
            name="combine",
        )(len_blk, ct, ys)

    return jax.shard_map(
        shard_body,
        mesh=mesh,
        in_specs=(P("data", "seq", None), P("data"), P(None, None), P(None), P("seq", None, None), P("seq", None, None)),
        out_specs=P("data", "seq", None),
        check_vma=False,
    )
```

time: 282 us -> 138 us (0.49)
  Pallas kernels: 0 us -> 137 us
  matrix products: 136 us -> 0 us
  waiting for transfers between devices: 55.6 us -> 0 us
  other arithmetic: 49.2 us -> 0 us
  blocking collectives: 23.5 us -> 0 us
  between operations: 14.1 us -> 0.66 us
  local copies, waits for them, and re-layouts: 2.96 us -> 0 us
    pallas_call x0 -> x2, Pallas kernels: none -> 137 us  [the longest x1 98.8 us: shard_body(): pl.pallas_call(functools.partial(_front_kernel, rows, experts), out_shape...]
    dot_general x5 -> x0, matrix products: 136 us -> none  [the longest x1 29.3 us: shard_body(): jnp.einsum('besd,edf->besf', slot_in, w_in_blk, preferred_element_type=jn...]
    reduce_scatter x1 -> x0, waiting for transfers between devices: 34 us -> none  [shard_body(): lax.psum_scatter(part_sum, 'seq', scatter_dimension=1, tiled=True)]
    reduce_sum x3 -> x0, other arithmetic: 25.1 us -> none  [the longest x1 17.1 us: shard_body(): jnp.sum(tok_f32 * tok_f32, axis=-1, keepdims=True) + 1e-06]
    sub x1 -> x0, other arithmetic: 22.2 us -> none  [shard_body(): combine_w = jax.nn.softmax(logits, axis=-1).astype(jnp.bfloat16)]
    all_gather x1 -> x0, waiting for transfers between devices: 21.6 us -> none  [shard_body(): all_out = lax.all_gather(slot_out, 'seq', axis=1, tiled=True)]
    pmax x1 -> x0, blocking collectives: 13 us -> none  [shard_body(): col_max = lax.pmax(local_max, 'seq')]
    psum x1 -> x0, blocking collectives: 10.4 us -> none  [shard_body(): col_sum = lax.psum(jnp.sum(disp_w, axis=1), 'seq')]
  transfers between devices with their start and end apart: 2 -> 0, of which waited for: 2 -> 0; matrix products, arithmetic and copies ran while one was open for 10% -> 0% of each run, Pallas kernels for 0% -> 0%
where the time goes in v1:
time: 138 us; the launch traced here: 137 us
  Pallas kernels  137 us (99%)
    pallas_call x1, Pallas kernels, shard_body(): pl.pallas_call(functools.partial(_front_kernel, rows, experts), out_shape...  98.8 us
    pallas_call x1, Pallas kernels, shard_body(): pl.pallas_call(_combine_kernel, grid_spec=pltpu.PrefetchScalarGridSpec(nu...  37.7 us

profile of v1, /device:TPU:0, one launch (start us, length us, event | category | flops | bytes accessed | tf_op | source)
XLA Modules:
  0.0 137.2 jit_solution(15809049671552002286)
XLA Ops:
  0.7 98.8 %front.1 = (bf16[128,32,768]{2,1,0:T(8,128)(2,1)}, bf16[32,128,1024]{2,1,0:T(8,128)(2,1)}) custom-call(s32[32]{0:T(128)} %len_ref.3, f32[1]{0:T(128)S(6)} %copy.7.scale_ref, bf16[768,128]{1,0:T(8,128)(2,1)} %phi_ref.1, bf16[32,1024,768]{2,1,0:T(8,128)(2,1)} %x_hbm.1, bf16[16,768,3072]{2,1,0:T(8,128)(2,1)} %win_hbm.1, bf16[16,3072,768]{2,1,0:T(8,128)(2,1)} %wout_hbm.1), custom_call_target="tpu_custom_call" | custom-call | tf_op jit(solution)/shard_map/front/pallas_call | solution.py:302
  99.5 37.7 %combine.1 = bf16[32,1024,768]{2,1,0:T(8,128)(2,1)} custom-call(s32[32]{0:T(128)} %len_ref.3, bf16[32,128,1024]{2,1,0:T(8,128)(2,1)} %get-tuple-element.7.ct_ref, bf16[128,32,768]{2,1,0:T(8,128)(2,1)} %get-tuple-element.8.ys_ref), custom_call_target="tpu_custom_call" | custom-call | tf_op jit(solution)/shard_map/combine/pallas_call | solution.py:332

commit v2 on v1

v2 whole, which is shorter than its diff:
```python
import functools

import jax
import jax.numpy as jnp
from jax import lax
from jax.experimental import pallas as pl
from jax.experimental.pallas import tpu as pltpu
from jax.sharding import PartitionSpec as P

BLK = 256
TS = 5
WS = 4
PARTS = 4
YS = 8
FC = 512
G = 16


def _swap_matrix():
    r = lax.broadcasted_iota(jnp.int32, (G * G, G * G), 0)
    c = lax.broadcasted_iota(jnp.int32, (G * G, G * G), 1)
    hit = ((r >> 4) == (c & 15)) & ((r & 15) == (c >> 4))
    return jnp.where(hit, 1.0, 0.0).astype(jnp.bfloat16)


def _front_kernel(rows, experts, len_ref, scale_ref, phi_hbm, x_hbm, win_hbm, wout_hbm,
                  ys_hbm, ct_hbm,
                  xbuf, phi_ref, phit, wt, ctst, sbuf, rbuf, qbuf, xst, zt, zr, zs, yst, w1, w2,
                  phi_sem, tok_sem, ct_sem, w_sem, z_ssem, z_rsem,
                  d_ssem, d_rsem, x_ssem, x_rsem,
                  l_sem, k_sem, c_ssem, c_rsem, p_ssem, p_rsem, f_ssem, f_rsem):
    toks, width = x_hbm.shape[1], x_hbm.shape[2]
    slots = phi_ref.shape[1]
    own = sbuf.shape[3]
    per = own // experts
    me = lax.axis_index("seq")
    xi = me // 2
    ci = me % 2
    core_peer = 2 * xi + (1 - ci)
    x_peer = 2 * (1 - xi) + ci
    diag = 2 * (1 - xi) + (1 - ci)

    def remote(src, dst, ssem, rsem, dev):
        return pltpu.make_async_remote_copy(
            src_ref=src, dst_ref=dst, send_sem=ssem, recv_sem=rsem,
            device_id={"seq": dev}, device_id_type=pl.DeviceIdType.MESH)

    def tok_copy(b):
        return pltpu.make_async_copy(x_hbm.at[b], xbuf.at[b % TS], tok_sem.at[b % TS])

    def ct_copy(b):
        return pltpu.make_async_copy(ctst.at[b % 2], ct_hbm.at[b], ct_sem.at[b % 2])

    def w1_copy(e):
        return pltpu.make_async_copy(win_hbm.at[e], w1.at[e % WS], w_sem.at[e % WS, 0])

    def w2_copy(e):
        return pltpu.make_async_copy(wout_hbm.at[e], w2.at[e % WS], w_sem.at[e % WS, 1])

    def w1_part(e, k):
        n = width // PARTS
        cut = pl.ds(pl.multiple_of(k * n, n), n)
        return pltpu.make_async_copy(win_hbm.at[e, cut], w1.at[e, cut], w_sem.at[e, 0])

    def w2_part(e, k):
        n = w2.shape[1] // PARTS
        cut = pl.ds(pl.multiple_of(k * n, n), n)
        return pltpu.make_async_copy(wout_hbm.at[e, cut], w2.at[e, cut], w_sem.at[e, 1])

    def d_copy(b):
        return remote(sbuf.at[b, :, 1 - ci], rbuf.at[b], d_ssem, d_rsem.at[b], core_peer)

    def x_copy(b):
        return remote(rbuf.at[b, 1 - xi], qbuf.at[b], x_ssem, x_rsem.at[b // G], x_peer)

    def z_copies():
        out = []
        for k, dev in enumerate((core_peer, x_peer, diag)):
            out.append(remote(zt.at[pl.ds(pl.multiple_of(dev * own, own), own)], zr.at[k],
                              z_ssem.at[k], z_rsem.at[k], dev))
        return out

    phi_copy = pltpu.make_async_copy(phi_hbm, phi_ref, phi_sem)
    phi_copy.start()
    for k in range(TS - 2):
        tok_copy(k).start()

    barrier = pltpu.get_barrier_semaphore()
    for dev in (core_peer, x_peer, diag):
        pl.semaphore_signal(barrier, inc=1, device_id={"seq": dev}, device_id_type=pl.DeviceIdType.MESH)

    phi_copy.wait()
    scale = scale_ref[0]
    phi = phi_ref[...].astype(jnp.float32)
    col_inv = lax.rsqrt(jnp.sum(phi * phi, axis=0, keepdims=True) + 1e-6)
    phit[...] = (phi * (scale * col_inv)).T.astype(jnp.bfloat16)
    zt[...] = jnp.zeros_like(zt)

    def gate(b):
        limit = len_ref[b] - me * toks
        zacc = None
        for k in range(toks // BLK):
            cols = pl.ds(k * BLK, BLK)
            xf = xbuf[b % TS, cols, :].astype(jnp.float32)
            inv = lax.rsqrt(jnp.sum(xf * xf, axis=1, keepdims=True) + 1e-6)
            xn = (xf * inv).astype(jnp.bfloat16)
            lt = lax.dot_general(phit[...], xn, (((1,), (1,)), ((), ())),
                                 preferred_element_type=jnp.float32)
            e = jnp.exp(lt - scale)
            den = jnp.sum(e, axis=0, keepdims=True)
            ctst[b % 2, :, cols] = (e * (1.0 / den)).astype(jnp.bfloat16)
            pos = lax.broadcasted_iota(jnp.int32, (1, BLK), 1) + k * BLK
            w = jnp.where(pos < limit, e, 0.0)
            wt[:, cols] = w.astype(jnp.bfloat16)
            for h in range(BLK // 128):
                part = w[:, h * 128:(h + 1) * 128]
                zacc = part if zacc is None else zacc + part
        zcol = jnp.sum(zacc, axis=1, keepdims=True)
        lane = lax.broadcasted_iota(jnp.int32, zt.shape, 1)
        zt[...] = jnp.where(lane == b, zcol, zt[...])

    def sums(b, slot):
        s = jnp.dot(wt[...], xbuf[slot], preferred_element_type=jnp.float32)
        sbuf[b] = s.astype(jnp.bfloat16).reshape(2, 2, own, width)

    def mid(b):
        for h in range(2):
            rbuf[b, h] = (rbuf[b, h].astype(jnp.float32)
                          + sbuf[b, h, ci].astype(jnp.float32)).astype(jnp.bfloat16)

    wt[...] = jnp.zeros_like(wt)
    pl.semaphore_wait(barrier, 3)

    def step(b, _):
        @pl.when(b >= 2)
        def _():
            d_copy(b - 2).start()
            ct_copy(b - 2).wait()

        @pl.when(b + TS - 2 < rows)
        def _():
            tok_copy(b + TS - 2).start()

        e, part = b // (2 * PARTS), b % PARTS

        @pl.when(b % (2 * PARTS) < PARTS)
        def _():
            w1_part(e, part).start()

        @pl.when(b % (2 * PARTS) >= PARTS)
        def _():
            w2_part(e, part).start()

        @pl.when(b >= 3)
        def _():
            d_copy(b - 3).wait_recv()
            mid(b - 3)

        tok_copy(b).wait()
        sums(jnp.maximum(b - 1, 0), (b + TS - 1) % TS)
        gate(b)
        ct_copy(b).start()

        @pl.when(b >= 3)
        def _():
            x_copy(b - 3).start()
        return 0

    lax.fori_loop(0, rows, step, 0)
    d_copy(rows - 2).start()
    zc = z_copies()
    for z in zc:
        z.start()
    sums(rows - 1, (rows - 1) % TS)
    d_copy(rows - 3).wait_recv()
    mid(rows - 3)
    d_copy(rows - 1).start()
    d_copy(rows - 2).wait_recv()
    mid(rows - 2)
    x_copy(rows - 3).start()
    d_copy(rows - 1).wait_recv()
    mid(rows - 1)
    x_copy(rows - 2).start()
    remote(rbuf, rbuf, d_ssem, d_rsem.at[0], core_peer).wait_send()
    ct_copy(rows - 2).wait()
    ct_copy(rows - 1).wait()
    x_copy(rows - 1).start()
    for z in zc:
        z.wait_recv()

    zs[...] = jnp.ones_like(zs)
    zs[:own, :] = zt[pl.ds(pl.multiple_of(me * own, own), own), :] + zr[0] + zr[1] + zr[2]
    zs[...] = 1.0 / zs[...].T

    swap = _swap_matrix()

    def settle(h, _):
        cut = pl.ds(pl.multiple_of(h * G, G), G)
        remote(qbuf.at[cut], qbuf.at[cut], x_ssem, x_rsem.at[h], x_peer).wait_recv()
        zi = zs[cut, :]
        for g in range(own // G):
            near = rbuf[cut, xi, pl.ds(g * G, G), :].reshape(G * G, width)
            far = qbuf[cut, pl.ds(g * G, G), :].reshape(G * G, width)
            s = (jnp.dot(swap, near, preferred_element_type=jnp.float32)
                 + jnp.dot(swap, far, preferred_element_type=jnp.float32))
            for k in range(G):
                zinv = zi[:, g * G + k:g * G + k + 1]
                xst[g * G + k, cut, :] = (s[k * G:(k + 1) * G] * zinv).astype(jnp.bfloat16)
        return 0

    lax.fori_loop(0, rows // G, settle, 0)

    def at(dev, e):
        return ys_hbm.at[pl.ds(dev * own + e * per, per)]

    def at_all(dev):
        return ys_hbm.at[pl.ds(dev * own, own)]

    def l_copy(e):
        return pltpu.make_async_copy(yst.at[e], at(me, e), l_sem)

    def c_copy(e):
        return remote(yst.at[e], at(me, e), c_ssem, c_rsem, core_peer)

    def p_copy(e):
        return remote(yst.at[e], sbuf.at[e, 0], p_ssem, p_rsem.at[e], x_peer)

    def f_copy(e):
        return remote(sbuf.at[e, 0], at(x_peer, e), f_ssem, f_rsem, core_peer)

    def k_copy(e):
        return pltpu.make_async_copy(sbuf.at[e, 0], at(x_peer, e), k_sem)

    def send(e):
        p_copy(e).start()
        c_copy(e).start()
        l_copy(e).start()

    def forward(e):
        p_copy(e).wait_recv()
        f_copy(e).start()
        k_copy(e).start()

    def expert(e, _):
        @pl.when(e >= 1)
        def _():
            send(e - 1)

        @pl.when(e >= 4)
        def _():
            forward(e - 4)

        w1_copy(e).wait()
        w2_copy(e).wait()
        slot = e % WS
        xs = xst[pl.ds(e * per, per)].reshape(per * rows, width)
        acc = None
        for f in range(w1.shape[2] // FC):
            hid = jnp.dot(xs, w1[slot, :, f * FC:(f + 1) * FC], preferred_element_type=jnp.float32)
            hid = jax.nn.gelu(hid).astype(jnp.bfloat16)
            part = jnp.dot(hid, w2[slot, f * FC:(f + 1) * FC, :], preferred_element_type=jnp.float32)
            acc = part if acc is None else acc + part
        yst[e] = acc.astype(jnp.bfloat16).reshape(per, rows, width)

        @pl.when(e + WS < experts)
        def _():
            w1_copy(e + WS).start()
            w2_copy(e + WS).start()

        return 0

    lax.fori_loop(0, experts, expert, 0)

    send(experts - 1)
    for e in range(experts - 4, experts):
        forward(e)
    remote(qbuf, qbuf, x_ssem, x_rsem.at[0], x_peer).wait_send()
    for z in zc:
        z.wait_send()
    mine, theirs = at_all(me), at_all(x_peer)
    remote(xst, mine, c_ssem, c_rsem, core_peer).wait()
    remote(xst, mine, p_ssem, p_rsem.at[0], x_peer).wait_send()
    remote(xst, theirs, f_ssem, f_rsem, core_peer).wait()
    pltpu.make_async_copy(xst, mine, l_sem).wait()
    pltpu.make_async_copy(xst, theirs, k_sem).wait()


def _combine_kernel(len_ref, ct_hbm, ys_hbm, y_hbm, ysv, ysb, ctb, yb, ys_sem, ct_sem, y_sem):
    rows, toks, width = y_hbm.shape
    slots = ys_hbm.shape[0]
    start = lax.axis_index("seq") * toks

    def ys_copy(h):
        return pltpu.make_async_copy(ys_hbm.at[:, pl.ds(pl.multiple_of(h * G, G), G)], ysv.at[h], ys_sem.at[h])

    def ct_copy(b):
        return pltpu.make_async_copy(ct_hbm.at[b], ctb.at[b % YS], ct_sem.at[b % YS])

    def y_copy(b):
        return pltpu.make_async_copy(yb.at[b % YS], y_hbm.at[b], y_sem.at[b % YS])

    ys_copy(0).start()
    for k in range(YS - 1):
        ct_copy(k).start()
    for h in range(1, rows // G):
        ys_copy(h).start()
    swap = _swap_matrix()

    def half(h, _):
        ys_copy(h).wait()
        for g in range(slots // G):
            blk = ysv[h, pl.ds(g * G, G)].reshape(G * G, width)
            out = jnp.dot(swap, blk, preferred_element_type=jnp.float32).astype(jnp.bfloat16)
            ysb[:, pl.ds(g * G, G), :] = out.reshape(G, G, width)

        def row(i, _):
            b = h * G + i

            @pl.when(b + YS - 1 < rows)
            def _():
                ct_copy(b + YS - 1).start()

            ct_copy(b).wait()

            @pl.when(b >= YS)
            def _():
                y_copy(b - YS).wait()

            limit = len_ref[b] - start

            @pl.when(limit > 0)
            def _():
                for k in range(toks // BLK):
                    c = ctb[b % YS, :, k * BLK:(k + 1) * BLK]
                    mixed = lax.dot_general(c, ysb[i], (((0,), (0,)), ((), ())),
                                            preferred_element_type=jnp.float32)
                    pos = lax.broadcasted_iota(jnp.int32, (BLK, 1), 0) + k * BLK
                    yb[b % YS, k * BLK:(k + 1) * BLK, :] = jnp.where(pos < limit, mixed, 0.0).astype(jnp.bfloat16)

            @pl.when(limit <= 0)
            def _():
                yb[b % YS] = jnp.zeros((toks, width), jnp.bfloat16)

            y_copy(b).start()
            return 0

        lax.fori_loop(0, G, row, 0)
        return 0

    lax.fori_loop(0, rows // G, half, 0)

    def finish(b, _):
        y_copy(b).wait()
        return 0
    lax.fori_loop(rows - YS, rows, finish, 0)


def solution(mesh):
    def shard_body(tok_blk, len_blk, slot_params, logit_scale, w_in_blk, w_out_blk):
        rows, toks, width = tok_blk.shape
        slots = slot_params.shape[1]
        experts, _, ff = w_in_blk.shape
        own = slots // mesh.shape["seq"]
        per = own // experts
        bf, f32 = jnp.bfloat16, jnp.float32
        any_spec = pl.BlockSpec(memory_space=pl.ANY)
        smem = pl.BlockSpec(memory_space=pltpu.SMEM)
        dma = pltpu.SemaphoreType.DMA
        ys, ct = pl.pallas_call(
            functools.partial(_front_kernel, rows, experts),
            out_shape=(jax.ShapeDtypeStruct((slots, rows, width), bf),
                       jax.ShapeDtypeStruct((rows, slots, toks), bf)),
            in_specs=[smem, smem, any_spec, any_spec, any_spec, any_spec],
            out_specs=(any_spec, any_spec),
            scratch_shapes=[
                pltpu.VMEM((TS, toks, width), bf),
                pltpu.VMEM((width, slots), bf),
                pltpu.VMEM((slots, width), bf),
                pltpu.VMEM((slots, toks), bf),
                pltpu.VMEM((2, slots, toks), bf),
                pltpu.VMEM((rows, 2, 2, own, width), bf),
                pltpu.VMEM((rows, 2, own, width), bf),
                pltpu.VMEM((rows, own, width), bf),
                pltpu.VMEM((own, rows, width), bf),
                pltpu.VMEM((slots, 128), f32),
                pltpu.VMEM((3, own, 128), f32),
                pltpu.VMEM((128, 128), f32),
                pltpu.VMEM((experts, per, rows, width), bf),
                pltpu.VMEM((WS, width, ff), bf),
                pltpu.VMEM((WS, ff, width), bf),
                dma, dma((TS,)), dma((2,)), dma((WS, 2)), dma((3,)), dma((3,)),
                dma, dma((rows,)), dma, dma((rows // G,)),
                dma, dma, dma, dma, dma, dma((experts,)), dma, dma,
            ],
            compiler_params=pltpu.CompilerParams(
                collective_id=0, has_side_effects=True, vmem_limit_bytes=67_000_000),
            name="front",
        )(len_blk, logit_scale, slot_params, tok_blk, w_in_blk, w_out_blk)
        return pl.pallas_call(
            _combine_kernel,
            in_specs=[smem, any_spec, any_spec],
            out_specs=any_spec,
            out_shape=jax.ShapeDtypeStruct((rows, toks, width), bf),
            scratch_shapes=[
                pltpu.VMEM((rows // G, slots, G, width), bf),
                pltpu.VMEM((G, slots, width), bf),
                pltpu.VMEM((YS, slots, toks), bf),
                pltpu.VMEM((YS, toks, width), bf),
                dma((rows // G,)), dma((YS,)), dma((YS,)),
            ],
            compiler_params=pltpu.CompilerParams(vmem_limit_bytes=60_000_000),
            name="combine",
        )(len_blk, ct, ys)

    return jax.shard_map(
        shard_body,
        mesh=mesh,
        in_specs=(P("data", "seq", None), P("data"), P(None, None), P(None), P("seq", None, None), P("seq", None, None)),
        out_specs=P("data", "seq", None),
        check_vma=False,
    )
```

time: 138 us -> 118 us (0.86)
  Pallas kernels: 137 us -> 118 us
    pallas_call x1, Pallas kernels: 37.7 us -> 26.2 us  [shard_body(): pl.pallas_call(_combine_kernel, in_specs=[smem, any_spec, any_spec], out_...]
    pallas_call x1, Pallas kernels: 98.8 us -> 91.4 us  [shard_body(): pl.pallas_call(functools.partial(_front_kernel, rows, experts), out_shape...]
where the time goes in v2:
time: 118 us
  Pallas kernels  118 us (100%)
    pallas_call x1, Pallas kernels, shard_body(): pl.pallas_call(functools.partial(_front_kernel, rows, experts), out_shape...  91.4 us
    pallas_call x1, Pallas kernels, shard_body(): pl.pallas_call(_combine_kernel, in_specs=[smem, any_spec, any_spec], out_...  26.2 us

profile of v2, /device:TPU:0, one launch (start us, length us, event | category | flops | bytes accessed | tf_op | source)
XLA Modules:
  0.0 118.3 jit_solution(12081935641724440804)
XLA Ops:
  0.7 91.4 %front.1 = (bf16[128,32,768]{2,1,0:T(8,128)(2,1)}, bf16[32,128,1024]{2,1,0:T(8,128)(2,1)}) custom-call(s32[32]{0:T(128)} %len_ref.3, f32[1]{0:T(128)S(6)} %copy.7.scale_ref, bf16[768,128]{1,0:T(8,128)(2,1)} %phi_hbm.1, bf16[32,1024,768]{2,1,0:T(8,128)(2,1)} %x_hbm.1, bf16[16,768,3072]{2,1,0:T(8,128)(2,1)} %win_hbm.1, bf16[16,3072,768]{2,1,0:T(8,128)(2,1)} %wout_hbm.1), custom_call_target="tpu_custom_call" | custom-call | tf_op jit(solution)/shard_map/front/pallas_call | solution.py:369
  92.1 26.2 %combine.1 = bf16[32,1024,768]{2,1,0:T(8,128)(2,1)} custom-call(s32[32]{0:T(128)} %len_ref.3, bf16[32,128,1024]{2,1,0:T(8,128)(2,1)} %get-tuple-element.7.ct_hbm, bf16[128,32,768]{2,1,0:T(8,128)(2,1)} %get-tuple-element.8.ys_hbm), custom_call_target="tpu_custom_call" | custom-call | tf_op jit(solution)/shard_map/combine/pallas_call | solution.py:399

commit v3 on v2

--- a/solution.py
+++ b/solution.py
@@ -8,11 +8,13 @@
 from jax.sharding import PartitionSpec as P
 
 BLK = 256
-TS = 5
-WS = 4
-PARTS = 4
+TS = 4
+SS = 8
+WS = 14
+FC = 1024
+FS = 1024
+LAG = 3
 YS = 8
-FC = 512
 G = 16
 
 
@@ -25,7 +27,7 @@
 
 def _front_kernel(rows, experts, len_ref, scale_ref, phi_hbm, x_hbm, win_hbm, wout_hbm,
                   ys_hbm, ct_hbm,
-                  xbuf, phi_ref, phit, wt, ctst, sbuf, rbuf, qbuf, xst, zt, zr, zs, yst, w1, w2,
+                  xbuf, phi_ref, phit, wt, ctst, sbuf, rbuf, qbuf, xst, zt, zr, zs, w1, w2,
                   phi_sem, tok_sem, ct_sem, w_sem, z_ssem, z_rsem,
                   d_ssem, d_rsem, x_ssem, x_rsem,
                   l_sem, k_sem, c_ssem, c_rsem, p_ssem, p_rsem, f_ssem, f_rsem):
@@ -33,6 +35,8 @@
     slots = phi_ref.shape[1]
     own = sbuf.shape[3]
     per = own // experts
+    units = win_hbm.shape[2] // FC
+    many = per * rows
     me = lax.axis_index("seq")
     xi = me // 2
     ci = me % 2
@@ -51,24 +55,16 @@
     def ct_copy(b):
         return pltpu.make_async_copy(ctst.at[b % 2], ct_hbm.at[b], ct_sem.at[b % 2])
 
-    def w1_copy(e):
-        return pltpu.make_async_copy(win_hbm.at[e], w1.at[e % WS], w_sem.at[e % WS, 0])
-
-    def w2_copy(e):
-        return pltpu.make_async_copy(wout_hbm.at[e], w2.at[e % WS], w_sem.at[e % WS, 1])
-
-    def w1_part(e, k):
-        n = width // PARTS
-        cut = pl.ds(pl.multiple_of(k * n, n), n)
-        return pltpu.make_async_copy(win_hbm.at[e, cut], w1.at[e, cut], w_sem.at[e, 0])
-
-    def w2_part(e, k):
-        n = w2.shape[1] // PARTS
-        cut = pl.ds(pl.multiple_of(k * n, n), n)
-        return pltpu.make_async_copy(wout_hbm.at[e, cut], w2.at[e, cut], w_sem.at[e, 1])
+    def w1_copy(u):
+        cols = pl.ds(pl.multiple_of(u % units * FC, FC), FC)
+        return pltpu.make_async_copy(win_hbm.at[u // units, :, cols], w1.at[u % WS], w_sem.at[u % WS, 0])
+
+    def w2_copy(u):
+        cut = pl.ds(pl.multiple_of(u % units * FC, FC), FC)
+        return pltpu.make_async_copy(wout_hbm.at[u // units, cut], w2.at[u % WS], w_sem.at[u % WS, 1])
 
     def d_copy(b):
-        return remote(sbuf.at[b, :, 1 - ci], rbuf.at[b], d_ssem, d_rsem.at[b], core_peer)
+        return remote(sbuf.at[b % SS, :, 1 - ci], rbuf.at[b], d_ssem.at[b % SS], d_rsem.at[b], core_peer)
 
     def x_copy(b):
         return remote(rbuf.at[b, 1 - xi], qbuf.at[b], x_ssem, x_rsem.at[b // G], x_peer)
@@ -121,12 +117,12 @@
 
     def sums(b, slot):
         s = jnp.dot(wt[...], xbuf[slot], preferred_element_type=jnp.float32)
-        sbuf[b] = s.astype(jnp.bfloat16).reshape(2, 2, own, width)
+        sbuf[b % SS] = s.astype(jnp.bfloat16).reshape(2, 2, own, width)
 
     def mid(b):
         for h in range(2):
             rbuf[b, h] = (rbuf[b, h].astype(jnp.float32)
-                          + sbuf[b, h, ci].astype(jnp.float32)).astype(jnp.bfloat16)
+                          + sbuf[b % SS, h, ci].astype(jnp.float32)).astype(jnp.bfloat16)
 
     wt[...] = jnp.zeros_like(wt)
     pl.semaphore_wait(barrier, 3)
@@ -141,15 +137,17 @@
         def _():
             tok_copy(b + TS - 2).start()
 
-        e, part = b // (2 * PARTS), b % PARTS
-
-        @pl.when(b % (2 * PARTS) < PARTS)
-        def _():
-            w1_part(e, part).start()
-
-        @pl.when(b % (2 * PARTS) >= PARTS)
-        def _():
-            w2_part(e, part).start()
+        @pl.when((b < 2 * WS) & (b % 2 == 0))
+        def _():
+            w1_copy(b // 2).start()
+
+        @pl.when((b < 2 * WS) & (b % 2 == 1))
+        def _():
+            w2_copy(b // 2).start()
+
+        @pl.when(b > SS)
+        def _():
+            d_copy(b - 1 - SS).wait_send()
 
         @pl.when(b >= 3)
         def _():
@@ -171,6 +169,7 @@
     zc = z_copies()
     for z in zc:
         z.start()
+    d_copy(rows - 1 - SS).wait_send()
     sums(rows - 1, (rows - 1) % TS)
     d_copy(rows - 3).wait_recv()
     mid(rows - 3)
@@ -181,7 +180,6 @@
     d_copy(rows - 1).wait_recv()
     mid(rows - 1)
     x_copy(rows - 2).start()
-    remote(rbuf, rbuf, d_ssem, d_rsem.at[0], core_peer).wait_send()
     ct_copy(rows - 2).wait()
     ct_copy(rows - 1).wait()
     x_copy(rows - 1).start()
@@ -210,26 +208,32 @@
 
     lax.fori_loop(0, rows // G, settle, 0)
 
+    for b in range(rows - SS, rows):
+        d_copy(b).wait_send()
+
     def at(dev, e):
-        return ys_hbm.at[pl.ds(dev * own + e * per, per)]
+        return ys_hbm.at[pl.ds(pl.multiple_of((dev * experts + e) * many, many), many)]
 
     def at_all(dev):
-        return ys_hbm.at[pl.ds(dev * own, own)]
+        return ys_hbm.at[pl.ds(pl.multiple_of(dev * experts * many, many), experts * many)]
+
+    def here(slot, e):
+        return xbuf.at[slot, pl.ds(pl.multiple_of(e * many, many), many)]
 
     def l_copy(e):
-        return pltpu.make_async_copy(yst.at[e], at(me, e), l_sem)
+        return pltpu.make_async_copy(here(0, e), at(me, e), l_sem)
 
     def c_copy(e):
-        return remote(yst.at[e], at(me, e), c_ssem, c_rsem, core_peer)
+        return remote(here(0, e), at(me, e), c_ssem, c_rsem, core_peer)
 
     def p_copy(e):
-        return remote(yst.at[e], sbuf.at[e, 0], p_ssem, p_rsem.at[e], x_peer)
+        return remote(here(0, e), here(1, e), p_ssem, p_rsem.at[e], x_peer)
 
     def f_copy(e):
-        return remote(sbuf.at[e, 0], at(x_peer, e), f_ssem, f_rsem, core_peer)
+        return remote(here(1, e), at(x_peer, e), f_ssem, f_rsem, core_peer)
 
     def k_copy(e):
-        return pltpu.make_async_copy(sbuf.at[e, 0], at(x_peer, e), k_sem)
+        return pltpu.make_async_copy(here(1, e), at(x_peer, e), k_sem)
 
     def send(e):
         p_copy(e).start()
@@ -246,43 +250,45 @@
         def _():
             send(e - 1)
 
-        @pl.when(e >= 4)
-        def _():
-            forward(e - 4)
-
-        w1_copy(e).wait()
-        w2_copy(e).wait()
-        slot = e % WS
-        xs = xst[pl.ds(e * per, per)].reshape(per * rows, width)
+        @pl.when(e >= LAG)
+        def _():
+            forward(e - LAG)
+
+        xs = xst[pl.ds(e * per, per)].reshape(many, width)
         acc = None
-        for f in range(w1.shape[2] // FC):
-            hid = jnp.dot(xs, w1[slot, :, f * FC:(f + 1) * FC], preferred_element_type=jnp.float32)
-            hid = jax.nn.gelu(hid).astype(jnp.bfloat16)
-            part = jnp.dot(hid, w2[slot, f * FC:(f + 1) * FC, :], preferred_element_type=jnp.float32)
-            acc = part if acc is None else acc + part
-        yst[e] = acc.astype(jnp.bfloat16).reshape(per, rows, width)
-
-        @pl.when(e + WS < experts)
-        def _():
-            w1_copy(e + WS).start()
-            w2_copy(e + WS).start()
-
+        for f in range(units):
+            u = e * units + f
+            slot = u % WS
+            w1_copy(u).wait()
+            w2_copy(u).wait()
+            for k in range(FC // FS):
+                cut = slice(k * FS, (k + 1) * FS)
+                hid = jnp.dot(xs, w1[slot, :, cut], preferred_element_type=jnp.float32)
+                hid = jax.nn.gelu(hid).astype(jnp.bfloat16)
+                part = jnp.dot(hid, w2[slot, cut, :], preferred_element_type=jnp.float32)
+                acc = part if acc is None else acc + part
+
+            @pl.when(u + WS < experts * units)
+            def _():
+                w1_copy(u + WS).start()
+                w2_copy(u + WS).start()
+
+        xbuf[0, pl.ds(pl.multiple_of(e * many, many), many)] = acc.astype(jnp.bfloat16)
         return 0
 
     lax.fori_loop(0, experts, expert, 0)
-
     send(experts - 1)
-    for e in range(experts - 4, experts):
+    for e in range(experts - LAG, experts):
         forward(e)
     remote(qbuf, qbuf, x_ssem, x_rsem.at[0], x_peer).wait_send()
     for z in zc:
         z.wait_send()
-    mine, theirs = at_all(me), at_all(x_peer)
-    remote(xst, mine, c_ssem, c_rsem, core_peer).wait()
-    remote(xst, mine, p_ssem, p_rsem.at[0], x_peer).wait_send()
-    remote(xst, theirs, f_ssem, f_rsem, core_peer).wait()
-    pltpu.make_async_copy(xst, mine, l_sem).wait()
-    pltpu.make_async_copy(xst, theirs, k_sem).wait()
+    mine, theirs, whole = at_all(me), at_all(x_peer), xbuf.at[0]
+    remote(whole, mine, c_ssem, c_rsem, core_peer).wait()
+    remote(whole, mine, p_ssem, p_rsem.at[0], x_peer).wait_send()
+    remote(whole, theirs, f_ssem, f_rsem, core_peer).wait()
+    pltpu.make_async_copy(whole, mine, l_sem).wait()
+    pltpu.make_async_copy(whole, theirs, k_sem).wait()
 
 
 def _combine_kernel(len_ref, ct_hbm, ys_hbm, y_hbm, ysv, ysb, ctb, yb, ys_sem, ct_sem, y_sem):
@@ -300,7 +306,7 @@
         return pltpu.make_async_copy(yb.at[b % YS], y_hbm.at[b], y_sem.at[b % YS])
 
     ys_copy(0).start()
-    for k in range(YS - 1):
+    for k in range(YS - 2):
         ct_copy(k).start()
     for h in range(1, rows // G):
         ys_copy(h).start()
@@ -313,38 +319,47 @@
             out = jnp.dot(swap, blk, preferred_element_type=jnp.float32).astype(jnp.bfloat16)
             ysb[:, pl.ds(g * G, G), :] = out.reshape(G, G, width)
 
-        def row(i, _):
-            b = h * G + i
-
-            @pl.when(b + YS - 1 < rows)
+        def pair(p, _):
+            first = h * G + 2 * p
+            limits = []
+            for j in range(2):
+                b = first + j
+
+                @pl.when(b + YS - 2 < rows)
+                def _():
+                    ct_copy(b + YS - 2).start()
+
+                ct_copy(b).wait()
+
+                @pl.when(b >= YS)
+                def _():
+                    y_copy(b - YS).wait()
+
+                limits.append(len_ref[b] - start)
+
+            @pl.when(jnp.maximum(limits[0], limits[1]) > 0)
             def _():
-                ct_copy(b + YS - 1).start()
-
-            ct_copy(b).wait()
-
-            @pl.when(b >= YS)
+                for j in range(2):
+                    slot = (first + j) % YS
+                    own = ysb[2 * p + j]
+                    for k in range(toks // BLK):
+                        c = ctb[slot, :, k * BLK:(k + 1) * BLK]
+                        mixed = lax.dot_general(c, own, (((0,), (0,)), ((), ())),
+                                                preferred_element_type=jnp.float32)
+                        pos = lax.broadcasted_iota(jnp.int32, (BLK, 1), 0) + k * BLK
+                        yb[slot, k * BLK:(k + 1) * BLK, :] = jnp.where(
+                            pos < limits[j], mixed, 0.0).astype(jnp.bfloat16)
+
+            @pl.when(jnp.maximum(limits[0], limits[1]) <= 0)
             def _():
-                y_copy(b - YS).wait()
-
-            limit = len_ref[b] - start
-
-            @pl.when(limit > 0)
-            def _():
-                for k in range(toks // BLK):
-                    c = ctb[b % YS, :, k * BLK:(k + 1) * BLK]
-                    mixed = lax.dot_general(c, ysb[i], (((0,), (0,)), ((), ())),
-                                            preferred_element_type=jnp.float32)
-                    pos = lax.broadcasted_iota(jnp.int32, (BLK, 1), 0) + k * BLK
-                    yb[b % YS, k * BLK:(k + 1) * BLK, :] = jnp.where(pos < limit, mixed, 0.0).astype(jnp.bfloat16)
-
-            @pl.when(limit <= 0)
-            def _():
-                yb[b % YS] = jnp.zeros((toks, width), jnp.bfloat16)
-
-            y_copy(b).start()
+                for j in range(2):
+                    yb[(first + j) % YS] = jnp.zeros((toks, width), jnp.bfloat16)
+
+            for j in range(2):
+                y_copy(first + j).start()
             return 0
 
-        lax.fori_loop(0, G, row, 0)
+        lax.fori_loop(0, G // 2, pair, 0)
         return 0
 
     lax.fori_loop(0, rows // G, half, 0)
@@ -368,7 +383,7 @@
         dma = pltpu.SemaphoreType.DMA
         ys, ct = pl.pallas_call(
             functools.partial(_front_kernel, rows, experts),
-            out_shape=(jax.ShapeDtypeStruct((slots, rows, width), bf),
+            out_shape=(jax.ShapeDtypeStruct((slots * rows, width), bf),
                        jax.ShapeDtypeStruct((rows, slots, toks), bf)),
             in_specs=[smem, smem, any_spec, any_spec, any_spec, any_spec],
             out_specs=(any_spec, any_spec),
@@ -378,18 +393,17 @@
                 pltpu.VMEM((slots, width), bf),
                 pltpu.VMEM((slots, toks), bf),
                 pltpu.VMEM((2, slots, toks), bf),
-                pltpu.VMEM((rows, 2, 2, own, width), bf),
+                pltpu.VMEM((SS, 2, 2, own, width), bf),
                 pltpu.VMEM((rows, 2, own, width), bf),
                 pltpu.VMEM((rows, own, width), bf),
                 pltpu.VMEM((own, rows, width), bf),
                 pltpu.VMEM((slots, 128), f32),
                 pltpu.VMEM((3, own, 128), f32),
                 pltpu.VMEM((128, 128), f32),
-                pltpu.VMEM((experts, per, rows, width), bf),
-                pltpu.VMEM((WS, width, ff), bf),
-                pltpu.VMEM((WS, ff, width), bf),
+                pltpu.VMEM((WS, width, FC), bf),
+                pltpu.VMEM((WS, FC, width), bf),
                 dma, dma((TS,)), dma((2,)), dma((WS, 2)), dma((3,)), dma((3,)),
-                dma, dma((rows,)), dma, dma((rows // G,)),
+                dma((SS,)), dma((rows,)), dma, dma((rows // G,)),
                 dma, dma, dma, dma, dma, dma((experts,)), dma, dma,
             ],
             compiler_params=pltpu.CompilerParams(
@@ -410,7 +424,7 @@
             ],
             compiler_params=pltpu.CompilerParams(vmem_limit_bytes=60_000_000),
             name="combine",
-        )(len_blk, ct, ys)
+        )(len_blk, ct, ys.reshape(slots, rows, width))
 
     return jax.shard_map(
         shard_body,

time: 118 us -> 115 us (0.975)
  Pallas kernels: 118 us -> 114 us
    pallas_call x1, Pallas kernels: 26.2 us -> 23.5 us  [shard_body(): pl.pallas_call(_combine_kernel, in_specs=[smem, any_spec, any_spec], out_...]
where the time goes in v3:
time: 115 us
  Pallas kernels  114 us (99%)
    pallas_call x1, Pallas kernels, shard_body(): pl.pallas_call(functools.partial(_front_kernel, rows, experts), out_shape...  90.7 us
    pallas_call x1, Pallas kernels, shard_body(): pl.pallas_call(_combine_kernel, in_specs=[smem, any_spec, any_spec], out_...  23.5 us

profile of v3, /device:TPU:0, one launch (start us, length us, event | category | flops | bytes accessed | tf_op | source)
XLA Modules:
  0.0 114.9 jit_solution(4488497339520290974)
XLA Ops:
  0.7 90.7 %front.1 = (bf16[4096,768]{1,0:T(8,128)(2,1)}, bf16[32,128,1024]{2,1,0:T(8,128)(2,1)}) custom-call(s32[32]{0:T(128)} %len_ref.3, f32[1]{0:T(128)S(6)} %copy.7.scale_ref, bf16[768,128]{1,0:T(8,128)(2,1)} %phi_hbm.1, bf16[32,1024,768]{2,1,0:T(8,128)(2,1)} %x_hbm.1, bf16[16,768,3072]{2,1,0:T(8,128)(2,1)} %win_hbm.1, bf16[16,3072,768]{2,1,0:T(8,128)(2,1)} %wout_hbm.1), custom_call_target="tpu_custom_call" | custom-call | tf_op jit(solution)/shard_map/front/pallas_call | solution.py:384
  91.4 23.5 %combine.1 = bf16[32,1024,768]{2,1,0:T(8,128)(2,1)} custom-call(s32[32]{0:T(128)} %len_ref.3, bf16[32,128,1024]{2,1,0:T(8,128)(2,1)} %get-tuple-element.7.ct_hbm, bf16[128,32,768]{2,1,0:T(8,128)(2,1)} %bitcast.1), custom_call_target="tpu_custom_call" | custom-call | tf_op jit(solution)/shard_map/combine/pallas_call | solution.py:413

commit v4 on v3

--- a/solution.py
+++ b/solution.py
@@ -10,7 +10,7 @@
 BLK = 256
 TS = 4
 SS = 8
-WS = 14
+WS = 12
 FC = 1024
 FS = 1024
 LAG = 3
@@ -128,9 +128,12 @@
     pl.semaphore_wait(barrier, 3)
 
     def step(b, _):
+        @pl.when(b >= 3)
+        def _():
+            x_copy(b - 3).start()
+
         @pl.when(b >= 2)
         def _():
-            d_copy(b - 2).start()
             ct_copy(b - 2).wait()
 
         @pl.when(b + TS - 2 < rows)
@@ -148,38 +151,35 @@
         @pl.when(b > SS)
         def _():
             d_copy(b - 1 - SS).wait_send()
-
-        @pl.when(b >= 3)
-        def _():
-            d_copy(b - 3).wait_recv()
-            mid(b - 3)
 
         tok_copy(b).wait()
         sums(jnp.maximum(b - 1, 0), (b + TS - 1) % TS)
         gate(b)
         ct_copy(b).start()
 
-        @pl.when(b >= 3)
-        def _():
-            x_copy(b - 3).start()
+        @pl.when(b >= 1)
+        def _():
+            d_copy(b - 1).start()
+
+        @pl.when(b >= 2)
+        def _():
+            d_copy(b - 2).wait_recv()
+            mid(b - 2)
         return 0
 
     lax.fori_loop(0, rows, step, 0)
-    d_copy(rows - 2).start()
+    x_copy(rows - 3).start()
     zc = z_copies()
     for z in zc:
         z.start()
     d_copy(rows - 1 - SS).wait_send()
     sums(rows - 1, (rows - 1) % TS)
-    d_copy(rows - 3).wait_recv()
-    mid(rows - 3)
-    d_copy(rows - 1).start()
     d_copy(rows - 2).wait_recv()
     mid(rows - 2)
-    x_copy(rows - 3).start()
+    d_copy(rows - 1).start()
+    x_copy(rows - 2).start()
     d_copy(rows - 1).wait_recv()
     mid(rows - 1)
-    x_copy(rows - 2).start()
     ct_copy(rows - 2).wait()
     ct_copy(rows - 1).wait()
     x_copy(rows - 1).start()

time: 115 us -> 115 us (level)
  no operation moved by 1% of the time
where the time goes in v4:
time: 115 us
  Pallas kernels  114 us (99%)
    pallas_call x1, Pallas kernels, shard_body(): pl.pallas_call(functools.partial(_front_kernel, rows, experts), out_shape...  90.5 us
    pallas_call x1, Pallas kernels, shard_body(): pl.pallas_call(_combine_kernel, in_specs=[smem, any_spec, any_spec], out_...  23.5 us

profile of v4, /device:TPU:0, one launch (start us, length us, event | category | flops | bytes accessed | tf_op | source)
XLA Modules:
  0.0 114.6 jit_solution(13566895473931019038)
XLA Ops:
  0.7 90.5 %front.1 = (bf16[4096,768]{1,0:T(8,128)(2,1)}, bf16[32,128,1024]{2,1,0:T(8,128)(2,1)}) custom-call(s32[32]{0:T(128)} %len_ref.3, f32[1]{0:T(128)S(6)} %copy.7.scale_ref, bf16[768,128]{1,0:T(8,128)(2,1)} %phi_hbm.1, bf16[32,1024,768]{2,1,0:T(8,128)(2,1)} %x_hbm.1, bf16[16,768,3072]{2,1,0:T(8,128)(2,1)} %win_hbm.1, bf16[16,3072,768]{2,1,0:T(8,128)(2,1)} %wout_hbm.1), custom_call_target="tpu_custom_call" | custom-call | tf_op jit(solution)/shard_map/front/pallas_call | solution.py:384
  91.1 23.5 %combine.1 = bf16[32,1024,768]{2,1,0:T(8,128)(2,1)} custom-call(s32[32]{0:T(128)} %len_ref.3, bf16[32,128,1024]{2,1,0:T(8,128)(2,1)} %get-tuple-element.7.ct_hbm, bf16[128,32,768]{2,1,0:T(8,128)(2,1)} %bitcast.1), custom_call_target="tpu_custom_call" | custom-call | tf_op jit(solution)/shard_map/combine/pallas_call | solution.py:413
